TPU v7x, 8 devices: a whole 2x2x1 slice. The times are simulated.
8 devices in a mesh: dp: 1 (over z), cp: 8 (over y, x, core).
Axes of the slice: x: 2, y: 2, z: 1, core: 2. Of those that a mesh axis runs over, the one named last changes fastest.
Arguments:
- x_in: bfloat16 [1024, 3072], P(('dp', 'cp'))
- d_y: bfloat16 [1024, 3072], P(('dp', 'cp'))
- w_q: bfloat16 [3072, 24, 128], replicated
- w_k: bfloat16 [3072, 8, 128], replicated
- w_v: bfloat16 [3072, 8, 128], replicated
- w_o: bfloat16 [24, 128, 3072], replicated
Outputs:
- output: bfloat16 [1024, 3072], P(('dp', 'cp'))
All inputs are finite; a program needn't handle non-finite values.
Results may differ from a plain program's by a relative error of at most 0.0114857.
Values are sent between devices in bfloat16 or wider.
A program may use at most 1 GiB of HBM per device.

v0:
```python
import math
import jax
import jax.numpy as jnp
from jax import lax
from jax.sharding import PartitionSpec as P


def block_rows(row_total, key_total, head_total):
    budget = max(1, 2 ** 23 // (key_total * head_total))
    return math.gcd(row_total, max(8, 2 ** int(math.log2(budget))))


def token_positions(row_ids, tok_len, n_dev):
    dev_idx = row_ids // tok_len
    row_off = row_ids % tok_len
    seg_len = tok_len // 2
    seg_idx = jnp.where(row_off < seg_len, dev_idx, 2 * n_dev - 1 - dev_idx)
    return seg_idx * seg_len + row_off % seg_len


def solution(mesh):
    n_dev = mesh.shape["cp"]
    row_spec = P(("dp", "cp"), None)

    def device_fn(x_in, d_y, w_q, w_k, w_v, w_o):
        tok_len, d_model = x_in.shape
        q_heads, head_dim = w_q.shape[1], w_q.shape[2]
        kv_heads = w_k.shape[1]
        q_group = q_heads // kv_heads
        seq_len = tok_len * n_dev
        score_scale = head_dim ** -0.5
        dev_rank = lax.axis_index("cp")
        wq_grp = w_q.reshape(d_model, kv_heads, q_group, head_dim)
        wo_grp = w_o.reshape(kv_heads, q_group, head_dim, d_model)
        q_loc = jnp.einsum("td,dkge->tkge", x_in, wq_grp, preferred_element_type=jnp.float32).astype(jnp.bfloat16)
        k_loc = jnp.einsum("td,dke->tke", x_in, w_k, preferred_element_type=jnp.float32).astype(jnp.bfloat16)
        v_loc = jnp.einsum("td,dke->tke", x_in, w_v, preferred_element_type=jnp.float32).astype(jnp.bfloat16)
        do_loc = jnp.einsum("td,kged->tkge", d_y, wo_grp, preferred_element_type=jnp.float32).astype(jnp.bfloat16)
        k_all = lax.all_gather(k_loc, "cp", axis=0, tiled=True)
        v_all = lax.all_gather(v_loc, "cp", axis=0, tiled=True)
        pos_all = token_positions(jnp.arange(seq_len), tok_len, n_dev)
        pos_loc = token_positions(dev_rank * tok_len + jnp.arange(tok_len), tok_len, n_dev)
        blk_rows = block_rows(tok_len, seq_len, q_heads)

        def block_step(acc_pair, blk_idx):
            dk_acc, dv_acc = acc_pair
            row_start = blk_idx * blk_rows
            q_blk = lax.dynamic_slice_in_dim(q_loc, row_start, blk_rows, 0)
            do_blk = lax.dynamic_slice_in_dim(do_loc, row_start, blk_rows, 0)
            pos_blk = lax.dynamic_slice_in_dim(pos_loc, row_start, blk_rows, 0)
            scores = jnp.einsum("rkge,ske->krgs", q_blk, k_all, preferred_element_type=jnp.float32) * score_scale
            causal = pos_blk[None, :, None, None] >= pos_all[None, None, None, :]
            scores = jnp.where(causal, scores, -jnp.inf)
            lse_blk = jax.nn.logsumexp(scores, axis=-1, keepdims=True)
            prob_blk = jnp.exp(scores - lse_blk).astype(jnp.bfloat16)
            out_blk = jnp.einsum("krgs,ske->krge", prob_blk, v_all, preferred_element_type=jnp.float32).astype(jnp.bfloat16)
            row_delta = jnp.einsum("rkge,krge->krg", do_blk, out_blk, preferred_element_type=jnp.float32)
            dp_blk = jnp.einsum("rkge,ske->krgs", do_blk, v_all, preferred_element_type=jnp.float32)
            ds_blk = (prob_blk * (dp_blk - row_delta[..., None])).astype(jnp.bfloat16)
            dq_blk = (jnp.einsum("krgs,ske->krge", ds_blk, k_all, preferred_element_type=jnp.float32) * score_scale).astype(jnp.bfloat16)
            dk_acc = dk_acc + jnp.einsum("krgs,rkge->kse", ds_blk, q_blk, preferred_element_type=jnp.float32)
            dv_acc = dv_acc + jnp.einsum("krgs,rkge->kse", prob_blk, do_blk, preferred_element_type=jnp.float32)
            return (dk_acc, dv_acc), dq_blk

        zero_acc = jnp.zeros((kv_heads, seq_len, head_dim), jnp.float32)
        (dk_part, dv_part), dq_blocks = lax.scan(block_step, (zero_acc, zero_acc), jnp.arange(tok_len // blk_rows))
        d_key = lax.psum_scatter(dk_part * score_scale, "cp", scatter_dimension=1, tiled=True).astype(jnp.bfloat16)
        d_value = lax.psum_scatter(dv_part, "cp", scatter_dimension=1, tiled=True).astype(jnp.bfloat16)
        d_x = jnp.einsum("bkrge,dkge->brd", dq_blocks, wq_grp, preferred_element_type=jnp.float32).reshape(tok_len, d_model)
        d_x = d_x + jnp.einsum("kte,dke->td", d_key, w_k, preferred_element_type=jnp.float32)
        d_x = d_x + jnp.einsum("kte,dke->td", d_value, w_v, preferred_element_type=jnp.float32)
        return d_x.astype(jnp.bfloat16)

    return jax.shard_map(device_fn, mesh=mesh, in_specs=(row_spec, row_spec, P(), P(), P(), P()), out_specs=row_spec, check_vma=False)
```

profile of v0, /device:TPU:0, one launch (start us, length us, event | category | flops | bytes accessed | tf_op | source)
XLA Modules:
  0.0 197.9 jit_solution(5827209734990008444)
XLA Ops:
  6.5 0.0 copy-start
  6.5 0.0 copy-start.6
  6.5 0.0 all-gather.3.cloned.1.call-start
  6.5 4.8 %fusion.45 = bf16[128,8,128]{2,0,1:T(8,128)(2,1)} fusion(bf16[3072,8,128]{2,1,0:T(8,128)(2,1)} %param.9, bf16[128,3072]{1,0:T(8,128)(2,1)} %param.6), kind=kOutput, calls=%fused_computation.36 | convolution fusion | flops 805437440 | bytes 7340032 | tf_op jit(solution)/shard_map/td,dke->tke/dot_general | solution.py:36
  11.4 0.0 all-gather.3.cloned.1.call-update
  11.4 0.0 all-gather.5.cloned.1.call-start
  11.5 0.0 copy-done.6
  11.5 4.5 %fusion.48 = bf16[128,8,128]{2,0,1:T(8,128)(2,1)} fusion(bf16[3072,8,128]{2,1,0:T(8,128)(2,1)} %param.10, bf16[128,3072]{1,0:T(8,128)(2,1)S(1)} %copy-done.6), kind=kOutput, calls=%fused_computation.37 | convolution fusion | flops 805437440 | bytes 7340032 | tf_op jit(solution)/shard_map/td,dke->tke/dot_general | solution.py:37
  16.0 0.0 all-gather.5.cloned.1.call-update
  16.0 0.0 reduce-scatter.3.cloned.1.call-start
  16.0 11.0 %copy.13 = bf16[3072,24,128]{2,0,1:T(8,128)(2,1)S(1)} copy(bf16[3072,24,128]{2,1,0:T(8,128)(2,1)} %param.8) | data formatting | bytes 37748736 | tf_op args[2]
  27.0 0.0 copy-start.2
  27.0 6.5 %copy-done.2 = bf16[3072,24,128]{2,0,1:T(8,128)(2,1)} copy-done((bf16[3072,24,128]{2,0,1:T(8,128)(2,1)}, bf16[3072,24,128]{2,0,1:T(8,128)(2,1)S(1)}, u32[]{:S(2)}) %copy-start.2) | copy-done | bytes 18874392
  33.5 2.6 %convolution_convert_fusion.1 = bf16[128,8,3,128]{3,0,2,1:T(8,128)(2,1)S(1)} fusion(bf16[3072,8,3,128]{3,0,2,1:T(8,128)(2,1)S(1)} %bitcast.70, bf16[128,3072]{1,0:T(8,128)(2,1)S(1)} %copy-done.6), kind=kOutput, calls=%fused_computation.35 | convolution fusion | flops 2416312320 | bytes 20447232 | tf_op jit(solution)/shard_map/td,dkge->tkge/dot_general | solution.py:35
  36.1 0.1 broadcast_compare_fusion
  36.3 0.0 copy-done
  36.3 11.3 %bitcast_convert_fusion = (f32[8,128,3,128]{3,1,2,0:T(8,128)}, bf16[128,8,3,128]{3,0,2,1:T(8,128)(2,1)S(1)}) fusion(bf16[8,3,128,3072]{3,2,1,0:T(8,128)(2,1)} %bitcast.72, bf16[128,3072]{1,0:T(8,128)(2,1)S(1)} %copy-done), kind=kOutput, calls=%fused_computation.42 | convolution fusion | flops 2416705536 | bytes 22020096 | tf_op jit(solution)/shard_map/td,kged->tkge/dot_general | solution.py:38
  47.6 0.0 all-gather.3.cloned.1.call-done
  47.6 3.7 %fusion.2 = (f32[8,128,3]{1,2,0:T(4,128)S(1)}, f32[8,128,3,1024]{3,1,2,0:T(8,128)S(1)}) fusion(pred[128,1024]{1,0:T(8,128)(4,1)S(1)} %broadcast_compare_fusion, bf16[128,8,3,128]{3,0,2,1:T(8,128)(2,1)S(1)} %convolution_convert_fusion.1, bf16[1024,8,128]{2,0,1:T(8,128)(2,1)} %all-gather.3.cloned.1.call-done), kind=kOutput, calls=%fused_computation.6 | convolution fusion | flops 814740480 | bytes 15609856 | tf_op jit(solution)/shard_map/while/body/eval_jaxpr/rkge,ske->krgs/dot_general | solution.py:51
  51.3 3.3 %exponential_reduce_fusion = f32[8,128,3]{1,2,0:T(4,128)S(1)} fusion(f32[8,128,3,1024]{3,1,2,0:T(8,128)S(1)} %get-tuple-element.24, f32[8,128,3]{1,2,0:T(4,128)S(1)} %is-finite_select_fusion, pred[128,1024]{1,0:T(8,128)(4,1)S(1)} %broadcast_compare_fusion), kind=kLoop, calls=%fused_computation.4 | loop fusion | flops 12579840 | bytes 12738560 | tf_op jit(solution)/shard_map/while/body/eval_jaxpr/reduce_sum | solution.py:54
  54.6 4.4 %exponential_convert_fusion = bf16[8,128,3,1024]{3,1,2,0:T(8,128)(2,1)} fusion(f32[8,128,3,1024]{3,1,2,0:T(8,128)S(1)} %get-tuple-element.24, f32[8,128,3]{1,2,0:T(4,128)S(1)} %log_add_fusion, pred[128,1024]{1,0:T(8,128)(4,1)S(1)} %broadcast_compare_fusion), kind=kLoop, calls=%fused_computation.3 | loop fusion | flops 12582912 | bytes 19017728 | tf_op jit(solution)/shard_map/while/body/eval_jaxpr/convert_element_type | solution.py:55
  59.0 1.2 all-gather.5.cloned.1.call-done
  60.2 0.0 copy-start.5
  60.2 5.3 %fusion.33 = bf16[8,128,3,128]{3,1,2,0:T(8,128)(2,1)S(1)} fusion(bf16[8,128,3,1024]{3,1,2,0:T(8,128)(2,1)} %exponential_convert_fusion, bf16[1024,8,128]{2,0,1:T(8,128)(2,1)} %all-gather.5.cloned.1.call-done), kind=kOutput, calls=%fused_computation.27 | convolution fusion | flops 805306368 | bytes 9175040 | tf_op jit(solution)/shard_map/while/body/eval_jaxpr/krgs,ske->krge/dot_general | solution.py:56
  65.5 0.0 copy-done.5
  65.5 1.7 multiply_reduce_fusion
  67.2 0.2 copy.29
  67.4 4.6 %multiply_convert_fusion = bf16[8,128,3,1024]{3,1,2,0:T(8,128)(2,1)S(1)} fusion(bf16[8,128,3,1024]{3,1,2,0:T(8,128)(2,1)} %exponential_convert_fusion, f32[8,128,3]{1,2,0:T(4,128)S(1)} %copy.29, bf16[128,8,3,128]{3,0,2,1:T(8,128)(2,1)S(1)} %get-tuple-element.26, bf16[1024,8,128]{2,0,1:T(8,128)(2,1)} %all-gather.5.cloned.1.call-done), kind=kOutput, calls=%fused_computation.2 | convolution fusion | flops 817889280 | bytes 15478784 | tf_op jit(solution)/shard_map/while/body/eval_jaxpr/rkge,ske->krgs/dot_general | solution.py:58
  72.0 0.0 copy-start.3
  72.0 2.6 %copy-done.3 = bf16[8,128,3,1024]{3,1,2,0:T(8,128)(2,1)} copy-done((bf16[8,128,3,1024]{3,1,2,0:T(8,128)(2,1)}, bf16[8,128,3,1024]{3,1,2,0:T(8,128)(2,1)S(1)}, u32[]{:S(2)}) %copy-start.3) | copy-done | bytes 6291480
  74.6 4.1 %bitcast_multiply_fusion = f32[8,1024,128]{2,1,0:T(8,128)} fusion(bf16[8,128,3,1024]{3,1,2,0:T(8,128)(2,1)S(1)} %multiply_convert_fusion, bf16[128,8,3,128]{3,0,2,1:T(8,128)(2,1)S(1)} %convolution_convert_fusion.1), kind=kOutput, calls=%fused_computation.17 | convolution fusion | flops 806354944 | bytes 11272192 | tf_op jit(solution)/shard_map/while/body/eval_jaxpr/krgs,rkge->kse/dot_general | solution.py:61
  78.6 0.0 reduce-scatter.3.cloned.1.call-update
  78.6 0.0 reduce-scatter.5.cloned.1.call-start
  78.7 6.7 %convolution_bitcast_fusion = f32[8,1024,128]{2,1,0:T(8,128)} fusion(bf16[8,128,3,1024]{3,1,2,0:T(8,128)(2,1)} %exponential_convert_fusion, bf16[128,8,3,128]{3,0,2,1:T(8,128)(2,1)S(1)} %get-tuple-element.26), kind=kOutput, calls=%fused_computation.24 | convolution fusion | flops 805306368 | bytes 11272192 | tf_op jit(solution)/shard_map/while/body/eval_jaxpr/krgs,rkge->kse/dot_general | solution.py:62
  85.4 0.0 reduce-scatter.5.cloned.1.call-update
  85.4 37.4 %reduce-scatter.3.cloned.1.call-done = f32[8,128,128]{2,1,0:T(8,128)} async-done(((f32[8,1024,128]{2,1,0:T(8,128)}), f32[8,128,128]{2,1,0:T(8,128)}) %reduce-scatter.3.cloned.1.call-update) | async-done | bytes 524304 | tf_op jit(solution)/shard_map/reduce_scatter | solution.py:67
  122.9 6.3 %fusion.13 = f32[128,3072]{1,0:T(8,128)} fusion(bf16[3072,8,128]{2,1,0:T(8,128)(2,1)} %param.9, f32[8,128,128]{2,1,0:T(8,128)} %reduce-scatter.3.cloned.1.call-done), kind=kOutput, calls=%fused_computation.18 | convolution fusion | flops 805437440 | bytes 8388608 | tf_op jit(solution)/shard_map/kte,dke->td/dot_general | solution.py:70
  129.2 0.0 copy-start.4
  129.2 39.3 %reduce-scatter.5.cloned.1.call-done = f32[8,128,128]{2,1,0:T(8,128)} async-done(((f32[8,1024,128]{2,1,0:T(8,128)}), f32[8,128,128]{2,1,0:T(8,128)}) %reduce-scatter.5.cloned.1.call-update) | async-done | bytes 524304 | tf_op jit(solution)/shard_map/reduce_scatter | solution.py:68
  168.5 6.3 %fusion.16 = f32[128,3072]{1,0:T(8,128)} fusion(bf16[3072,8,128]{2,1,0:T(8,128)(2,1)} %param.10, f32[8,128,128]{2,1,0:T(8,128)} %reduce-scatter.5.cloned.1.call-done), kind=kOutput, calls=%fused_computation.19 | convolution fusion | flops 805437440 | bytes 8388608 | tf_op jit(solution)/shard_map/kte,dke->td/dot_general | solution.py:71
  174.8 0.0 copy-done.4
  174.8 0.0 copy-start.1
  174.8 16.5 %fusion.28 = bf16[128,3072]{1,0:T(8,128)(2,1)} fusion(f32[128,3072]{1,0:T(8,128)} %fusion.16, f32[128,3072]{1,0:T(8,128)} %fusion.13, bf16[3072,8,3,128]{3,0,2,1:T(8,128)(2,1)} %bitcast.71, bf16[1024,8,128]{2,0,1:T(8,128)(2,1)S(1)} %copy-done.4, bf16[8,128,3,1024]{3,1,2,0:T(8,128)(2,1)} %copy-done.3), kind=kOutput, calls=%fused_computation.23 | convolution fusion | flops 3223191552 | bytes 31195136 | tf_op jit(solution)/shard_map/bkrge,dkge->brd/dot_general | solution.py:69
  191.3 0.0 copy-done.1
  (4 shorter events, 0.0 us)
Async XLA Ops:
  6.5 29.8 %copy-start = (bf16[128,3072]{1,0:T(8,128)(2,1)S(1)}, bf16[128,3072]{1,0:T(8,128)(2,1)}, u32[]{:S(2)}) copy-start(bf16[128,3072]{1,0:T(8,128)(2,1)} %param.7) | copy-start | bytes 2359300
  6.5 4.9 %copy-start.6 = (bf16[128,3072]{1,0:T(8,128)(2,1)S(1)}, bf16[128,3072]{1,0:T(8,128)(2,1)}, u32[]{:S(2)}) copy-start(bf16[128,3072]{1,0:T(8,128)(2,1)} %param.6) | copy-start | bytes 2359300
  6.5 41.1 %all-gather.3.cloned.1.call-start = ((), (), s32[]{:S(2)}) async-start(), calls=%async_computation.2 | async-start | bytes 2359296 | tf_op jit(solution)/shard_map/all_gather | solution.py:39
  11.4 48.8 %all-gather.5.cloned.1.call-start = ((), (), s32[]{:S(2)}) async-start(), calls=%async_computation.3 | async-start | bytes 2359296 | tf_op jit(solution)/shard_map/all_gather | solution.py:40
  16.0 106.9 %reduce-scatter.3.cloned.1.call-start = ((), (), s32[]{:S(2)}) async-start(), calls=%async_computation.4 | async-start | bytes 4718592 | tf_op jit(solution)/shard_map/reduce_scatter | solution.py:67
  27.0 6.5 %copy-start.2 = (bf16[3072,24,128]{2,0,1:T(8,128)(2,1)}, bf16[3072,24,128]{2,0,1:T(8,128)(2,1)S(1)}, u32[]{:S(2)}) copy-start(bf16[3072,24,128]{2,0,1:T(8,128)(2,1)S(1)} %copy.13) | copy-start | bytes 56623108
  60.2 5.3 %copy-start.5 = (f32[8,128,3,128]{3,1,2,0:T(8,128)S(1)}, f32[8,128,3,128]{3,1,2,0:T(8,128)}, u32[]{:S(2)}) copy-start(f32[8,128,3,128]{3,1,2,0:T(8,128)} %get-tuple-element.25) | copy-start | bytes 4718596
  72.0 2.6 %copy-start.3 = (bf16[8,128,3,1024]{3,1,2,0:T(8,128)(2,1)}, bf16[8,128,3,1024]{3,1,2,0:T(8,128)(2,1)S(1)}, u32[]{:S(2)}) copy-start(bf16[8,128,3,1024]{3,1,2,0:T(8,128)(2,1)S(1)} %multiply_convert_fusion) | copy-start | bytes 18874372
  78.6 89.9 %reduce-scatter.5.cloned.1.call-start = ((), (), s32[]{:S(2)}) async-start(), calls=%async_computation.5 | async-start | bytes 4718592 | tf_op jit(solution)/shard_map/reduce_scatter | solution.py:68
  129.2 45.6 %copy-start.4 = (bf16[1024,8,128]{2,0,1:T(8,128)(2,1)S(1)}, bf16[1024,8,128]{2,0,1:T(8,128)(2,1)}, u32[]{:S(2)}) copy-start(bf16[1024,8,128]{2,0,1:T(8,128)(2,1)} %all-gather.3.cloned.1.call-done) | copy-start | bytes 6291460
  174.8 16.5 %copy-start.1 = (bf16[128,3072]{1,0:T(8,128)(2,1)S(1)}, bf16[128,3072]{1,0:T(8,128)(2,1)}, u32[]{:S(2)}) copy-start(bf16[128,3072]{1,0:T(8,128)(2,1)} %param.7) | copy-start | bytes 2359300
Sparse Core Ops, SparseCore 0:
  11.5 24.7 all-gather.2
  38.2 21.9 all-gather.4
  78.8 44.0 reduce-scatter.2
  126.0 42.4 reduce-scatter.4
where the time goes:
time: 198 us
  waiting for transfers between devices  78 us (39%)
  matrix products  76.8 us (39%)
  local copies, waits for them, and re-layouts  20.2 us (10%)
  between operations  13.3 us (7%)
  other arithmetic  9.54 us (5%)
    reduce_scatter x1, waiting for transfers between devices, device_fn(): lax.psum_scatter(dv_part, 'cp', scatter_dimension=1, tiled=True)  39.3 us
    reduce_scatter x1, waiting for transfers between devices, device_fn(): lax.psum_scatter(dk_part * score_scale, 'cp', scatter_dimension=1, tiled=...  37.4 us
    unnamed x15, local copies, waits for them, and re-layouts  20 us
    dot_general x1, matrix products, device_fn(): jnp.einsum('bkrge,dkge->brd', dq_blocks, wq_grp, preferred_element_type=j...  16.5 us
    dot_general x1, matrix products, device_fn(): jnp.einsum('td,kged->tkge', d_y, wo_grp, preferred_element_type=jnp.float32)  11.3 us
    dot_general x1, matrix products, block_step(): jnp.einsum('krgs,rkge->kse', prob_blk, do_blk, preferred_element_type=jnp...  6.73 us
    dot_general x1, matrix products, device_fn(): jnp.einsum('kte,dke->td', d_key, w_k, preferred_element_type=jnp.float32)  6.33 us
    dot_general x1, matrix products, device_fn(): jnp.einsum('kte,dke->td', d_value, w_v, preferred_element_type=jnp.float32)  6.32 us
  transfers between devices with their start and end apart: 4, of which 3 were waited for; matrix products, arithmetic and copies ran while one was open for 27% of the time, Pallas kernels for 0%

commit v1 on v0

v1 whole, which is shorter than its diff:
```python
import functools
import math

import jax
import jax.numpy as jnp
from jax import lax
from jax.experimental import pallas as pl
from jax.experimental.pallas import tpu as pltpu
from jax.sharding import PartitionSpec as P

MESH = pl.DeviceIdType.MESH
BF16, F32 = jnp.bfloat16, jnp.float32
NT = (((1,), (1,)), ((), ()))

N_DEV, TOK, SEG = 8, 128, 64
SEQ = N_DEV * TOK
D = 3072
HD = 128
HQ, HKV, G = 24, 8, 3
BQ = 256
NB = SEQ // BQ
C = HD**-0.5
C2 = C * math.log2(math.e)
WO_SLOTS, W_SLOTS = 4, 4
U_DO, U_K, U_V, U_Q = 0, 3, 4, 5


def dot_nt(a, b):
    return lax.dot_general(a, b, NT, preferred_element_type=F32)


def dot(a, b):
    return jnp.dot(a, b, preferred_element_type=F32)


def kernel(x_hbm, dy_hbm, wq_hbm, wk_hbm, wv_hbm, wo_hbm, out_hbm,
           x_v, dy_v, wo_s, w_s, wrel, sbuf, recv, obuf, rin, acc, res,
           s_scr, p_scr, ds_scr, kt, vt, dk_acc, dv_acc,
           io_sem, wo_sem, w_sem, send_sem, recv_sem, osend_sem, orecv_sem, out_sem):
    me = lax.axis_index("cp")
    dp = lax.axis_index("dp")
    chip = me // 2

    barrier = pltpu.get_barrier_semaphore()
    for p in range(1, N_DEV):
        pl.semaphore_signal(barrier, inc=1, device_id=(dp, lax.rem(me + p, N_DEV)), device_id_type=MESH)

    x_cp = pltpu.make_async_copy(x_hbm, x_v, io_sem.at[0])
    dy_cp = pltpu.make_async_copy(dy_hbm, dy_v, io_sem.at[1])

    def wo_copy(s):
        cc = lax.rem(chip + s % 4 + 1, 4)
        slot = s % WO_SLOTS
        return pltpu.make_async_copy(wo_hbm.at[pl.ds(2 * cc, 2), s // 4], wo_s.at[slot], wo_sem.at[slot])

    def wkv_copy(w_hbm, i, slot):
        return pltpu.make_async_copy(w_hbm.at[pl.ds(i * 3, 3)], w_s.at[slot], w_sem.at[slot])

    def wq_copy(i, slot):
        return pltpu.make_async_copy(wq_hbm.at[i], w_s.at[slot], w_sem.at[slot])

    dy_cp.start()
    for s in range(WO_SLOTS):
        wo_copy(s).start()
    x_cp.start()
    for i in range(4):
        wkv_copy(wk_hbm, i, i).start()
    dk_acc[...] = jnp.zeros_like(dk_acc)
    dv_acc[...] = jnp.zeros_like(dv_acc)

    def send_block(unit, dest, val):
        @pl.when(dest != me)
        def _():
            sbuf[unit, dest] = val
            for half, seg in ((0, me), (1, 2 * N_DEV - 1 - me)):
                pltpu.make_async_remote_copy(
                    src_ref=sbuf.at[unit, dest, pl.ds(half * SEG, SEG)],
                    dst_ref=recv.at[unit, pl.ds(pl.multiple_of(seg * SEG, SEG), SEG)],
                    send_sem=send_sem, recv_sem=recv_sem.at[unit],
                    device_id=(dp, dest), device_id_type=MESH).start()

        @pl.when(dest == me)
        def _():
            recv[unit, pl.ds(pl.multiple_of(me * SEG, SEG), SEG), :] = val[:SEG]
            recv[unit, pl.ds(pl.multiple_of((2 * N_DEV - 1 - me) * SEG, SEG), SEG), :] = val[SEG:]

    dy_cp.wait()
    pl.semaphore_wait(barrier, N_DEV - 1)

    def do_step(s, _):
        cc = lax.rem(chip + s % 4 + 1, 4)
        slot = s % WO_SLOTS
        wo_copy(s).wait()
        w = wo_s[slot].reshape(2 * HD, D)
        val = dot_nt(dy_v[...], w).astype(BF16)
        for q in range(2):
            send_block(U_DO + s // 4, 2 * cc + q, val[:, q * HD:(q + 1) * HD])

        @pl.when(s + WO_SLOTS < 12)
        def _():
            wo_copy(s + WO_SLOTS).start()
        return 0

    lax.fori_loop(0, 12, do_step, 0)
    x_cp.wait()

    def relayout_kv(base, w_hbm, nxt, i, _):
        slot = i
        wkv_copy(w_hbm, i, slot).wait()
        blk = w_s[slot].reshape(3 * 256, 8, HD)
        wrel[pl.ds(base, 8), pl.ds(pl.multiple_of(i * 768, 768), 768), :] = jnp.swapaxes(blk, 0, 1)
        nxt(i, slot)
        return 0

    lax.fori_loop(0, 4, functools.partial(relayout_kv, HQ, wk_hbm, lambda i, slot: wkv_copy(wv_hbm, i, slot).start()), 0)
    lax.fori_loop(0, 4, functools.partial(relayout_kv, HQ + HKV, wv_hbm, lambda i, slot: wq_copy(i, slot).start()), 0)

    def kv_step(s, _):
        cc = lax.rem(chip + s % 4 + 1, 4)
        h0 = HQ + 8 * (s // 4) + 2 * cc
        w = jnp.concatenate([wrel[h0], wrel[h0 + 1]], axis=1)
        val = dot(x_v[...], w).astype(BF16)
        for q in range(2):
            send_block(U_K + s // 4, 2 * cc + q, val[:, q * HD:(q + 1) * HD])
        return 0

    lax.fori_loop(0, 8, kv_step, 0)

    def relayout_q(i, _):
        slot = i % W_SLOTS
        wq_copy(i, slot).wait()
        for t in range(3):
            wrel[pl.ds(8 * t, 8), pl.ds(pl.multiple_of(i * 256, 256), 256), :] = jnp.swapaxes(
                w_s[slot].reshape(256, 3, 8, HD)[:, t], 0, 1)

        @pl.when(i + W_SLOTS < 12)
        def _():
            wq_copy(i + W_SLOTS, slot).start()
        return 0

    lax.fori_loop(0, 12, relayout_q, 0)

    def q_step(s, _):
        cc = lax.rem(chip + s % 4 + 1, 4)
        g = s // 4
        h0 = 6 * cc + g
        w = jnp.concatenate([wrel[h0], wrel[h0 + 3]], axis=1)
        val = dot(x_v[...], w).astype(BF16)
        for q in range(2):
            send_block(U_Q + g, 2 * cc + q, val[:, q * HD:(q + 1) * HD])
        return 0

    lax.fori_loop(0, 12, q_step, 0)

    def wait_unit(u):
        part = recv.at[u, pl.ds(0, SEQ - TOK)]
        pltpu.make_async_copy(part, part, recv_sem.at[u]).wait()

    wait_unit(U_K)
    wait_unit(U_V)
    kt[...] = recv[U_K].T
    vt[...] = recv[U_V].T

    def send_out(u, head, seg):
        dest, half = (seg, 0) if seg < N_DEV else (2 * N_DEV - 1 - seg, 1)
        rows = pl.ds(seg * SEG, SEG)

        @pl.when(dest != me)
        def _():
            pltpu.make_async_remote_copy(
                src_ref=obuf.at[u, rows], dst_ref=rin.at[head, pl.ds(half * SEG, SEG)],
                send_sem=osend_sem, recv_sem=orecv_sem.at[u],
                device_id=(dp, dest), device_id_type=MESH).start()

        @pl.when(dest == me)
        def _():
            rin[head, half * SEG:(half + 1) * SEG, :] = obuf[u, rows, :]

    def attn_head(g, _):
        wait_unit(U_DO + g)
        wait_unit(U_Q + g)
        for b in reversed(range(NB)):
            n = (b + 1) * BQ
            rows = slice(b * BQ, (b + 1) * BQ)
            qb = recv[U_Q + g, rows, :]
            dob = recv[U_DO + g, rows, :]
            mx = None
            for kc in range(b + 1):
                ks = slice(kc * BQ, (kc + 1) * BQ)
                s = dot_nt(recv[U_K, ks, :], qb)
                if kc == b:
                    key = lax.broadcasted_iota(jnp.int32, (BQ, BQ), 0)
                    qry = lax.broadcasted_iota(jnp.int32, (BQ, BQ), 1)
                    s = jnp.where(key <= qry, s, -jnp.inf)
                s_scr[ks, :] = s
                mc = jnp.max(s.reshape(BQ // 8, 8, BQ), axis=0)
                mx = mc if mx is None else jnp.maximum(mx, mc)
            m2 = jnp.max(mx, axis=0, keepdims=True) * C2
            ls = None
            for kc in range(b + 1):
                ks = slice(kc * BQ, (kc + 1) * BQ)
                e = jnp.exp2(s_scr[ks, :] * C2 - m2)
                lc = jnp.sum(e.reshape(BQ // 8, 8, BQ), axis=0)
                ls = lc if ls is None else ls + lc
            lse2 = m2 + jnp.log2(jnp.sum(ls, axis=0, keepdims=True))
            for kc in range(b + 1):
                ks = slice(kc * BQ, (kc + 1) * BQ)
                p_scr[ks, :] = jnp.exp2(s_scr[ks, :] * C2 - lse2).astype(BF16)
            ot = dot(vt[:, :n], p_scr[:n, :]).astype(BF16)
            dot_t = dob.T
            delta = jnp.sum(dot_t.astype(F32) * ot.astype(F32), axis=0, keepdims=True)
            for kc in range(b + 1):
                ks = slice(kc * BQ, (kc + 1) * BQ)
                dpt = dot_nt(recv[U_V, ks, :], dob)
                ds = (p_scr[ks, :].astype(F32) * (dpt - delta)).astype(BF16)
                ds_scr[ks, :] = ds
                dk_acc[ks, :] += dot(ds, qb)
                dv_acc[ks, :] += dot(p_scr[ks, :], dob)
            dqt = (dot(kt[:, :n], ds_scr[:n, :]) * C).astype(BF16)
            obuf[g, rows, :] = dqt.T
            for i in range(BQ // SEG):
                send_out(g, G * me + g, b * (BQ // SEG) + i)

            @pl.when(g == G - 1)
            def _():
                obuf[3, rows, :] = (dk_acc[rows, :] * C).astype(BF16)
                obuf[4, rows, :] = dv_acc[rows, :].astype(BF16)
                for i in range(BQ // SEG):
                    send_out(3, HQ + me, b * (BQ // SEG) + i)
                    send_out(4, HQ + HKV + me, b * (BQ // SEG) + i)
        return 0

    lax.fori_loop(0, G, attn_head, 0)

    ND = 512
    for u in range(5):
        part = obuf.at[u, pl.ds(0, SEQ - TOK)]
        pltpu.make_async_copy(part, part, orecv_sem.at[u]).wait()
        heads = [G * j + u for j in range(8)] if u < 3 else [HQ + 8 * (u - 3) + j for j in range(8)]

        def dx_step(i, _, u=u, heads=heads):
            cols = pl.ds(pl.multiple_of(i * ND, ND), ND)
            lhs = jnp.concatenate([rin[h] for h in heads], axis=1)
            rhs = jnp.concatenate([wrel[h, cols, :] for h in heads], axis=1)
            t = dot_nt(lhs, rhs)
            if u > 0:
                t = t + acc[:, cols]
            if u < 4:
                acc[:, cols] = t
            else:
                res[:, cols] = t.astype(BF16)
                pltpu.make_async_copy(res.at[:, cols], out_hbm.at[:, cols], out_sem).start()
            return 0

        lax.fori_loop(0, D // ND, dx_step, 0)

    part = sbuf.at[pl.ds(0, 7)]
    pltpu.make_async_copy(part, part, send_sem).wait()
    part = obuf.at[:, pl.ds(0, SEQ - TOK)]
    pltpu.make_async_copy(part, part, osend_sem).wait()
    pltpu.make_async_copy(res, out_hbm, out_sem).wait()


def solution(mesh):
    row_spec = P(("dp", "cp"), None)

    def device_fn(x_in, d_y, w_q, w_k, w_v, w_o):
        dma = pltpu.SemaphoreType.DMA
        return pl.pallas_call(
            kernel,
            out_shape=jax.ShapeDtypeStruct((TOK, D), BF16),
            in_specs=[pl.BlockSpec(memory_space=pl.ANY)] * 6,
            out_specs=pl.BlockSpec(memory_space=pl.ANY),
            scratch_shapes=[
                pltpu.VMEM((TOK, D), BF16),
                pltpu.VMEM((TOK, D), BF16),
                pltpu.VMEM((WO_SLOTS, 2, HD, D), BF16),
                pltpu.VMEM((W_SLOTS, 3, 256, 8, HD), BF16),
                pltpu.VMEM((HQ + 2 * HKV, D, HD), BF16),
                pltpu.VMEM((8, N_DEV, TOK, HD), BF16),
                pltpu.VMEM((8, SEQ, HD), BF16),
                pltpu.VMEM((5, SEQ, HD), BF16),
                pltpu.VMEM((HQ + 2 * HKV, TOK, HD), BF16),
                pltpu.VMEM((TOK, D), F32),
                pltpu.VMEM((TOK, D), BF16),
                pltpu.VMEM((SEQ, BQ), F32),
                pltpu.VMEM((SEQ, BQ), BF16),
                pltpu.VMEM((SEQ, BQ), BF16),
                pltpu.VMEM((HD, SEQ), BF16),
                pltpu.VMEM((HD, SEQ), BF16),
                pltpu.VMEM((SEQ, HD), F32),
                pltpu.VMEM((SEQ, HD), F32),
                dma((2,)), dma((WO_SLOTS,)), dma((W_SLOTS,)),
                dma, dma((8,)), dma, dma((5,)), dma,
            ],
            compiler_params=pltpu.CompilerParams(
                collective_id=0, has_side_effects=True, vmem_limit_bytes=67_043_328),
        )(x_in, d_y, w_q.reshape(12, 3, 256, 8, HD),
          w_k.reshape(12, 256, 8, HD), w_v.reshape(12, 256, 8, HD),
          w_o.reshape(8, 3, HD, D))

    return jax.shard_map(device_fn, mesh=mesh, in_specs=(row_spec, row_spec, P(), P(), P(), P()),
                         out_specs=row_spec, check_vma=False)
```

time: 198 us -> 66.8 us (0.34)
  waiting for transfers between devices: 78 us -> 0 us
  matrix products: 76.8 us -> 0 us
  Pallas kernels: 0 us -> 64.6 us
  local copies, waits for them, and re-layouts: 20.2 us -> 2.06 us
  between operations: 13.3 us -> 0.01 us
  other arithmetic: 9.54 us -> 0 us
    dot_general x12 -> x0, matrix products: 76.8 us -> none  [the longest x1 16.5 us: device_fn(): jnp.einsum('bkrge,dkge->brd', dq_blocks, wq_grp, preferred_element_type=j...]
    reduce_scatter x2 -> x0, waiting for transfers between devices: 76.7 us -> none  [the longest x1 39.3 us: device_fn(): lax.psum_scatter(dv_part, 'cp', scatter_dimension=1, tiled=True)]
    pallas_call x0 -> x1, Pallas kernels: none -> 64.6 us  [device_fn(): pl.pallas_call(kernel, out_shape=jax.ShapeDtypeStruct((TOK, D), BF16), in...]
    unnamed x15 -> x1, local copies, waits for them, and re-layouts: 20 us -> 2.06 us
    convert_element_type x1 -> x0, other arithmetic: 4.37 us -> none  [block_step(): prob_blk = jnp.exp(scores - lse_blk).astype(jnp.bfloat16)]
    reduce_sum x1 -> x0, other arithmetic: 3.29 us -> none  [block_step(): lse_blk = jax.nn.logsumexp(scores, axis=-1, keepdims=True)]
  transfers between devices with their start and end apart: 4 -> 0, of which waited for: 3 -> 0; matrix products, arithmetic and copies ran while one was open for 27% -> 0% of each run, Pallas kernels for 0% -> 0%
where the time goes in v1:
time: 66.8 us; the launch traced here: 66.6 us
  Pallas kernels  64.6 us (97%)
  local copies, waits for them, and re-layouts  2.06 us (3%)
    pallas_call x1, Pallas kernels, device_fn(): pl.pallas_call(kernel, out_shape=jax.ShapeDtypeStruct((TOK, D), BF16), in...  64.6 us
    unnamed x1, local copies, waits for them, and re-layouts  2.06 us

profile of v1, /device:TPU:0, one launch (start us, length us, event | category | flops | bytes accessed | tf_op | source)
XLA Modules:
  0.0 66.6 jit_solution(6916192724996126617)
XLA Ops:
  0.0 64.6 %shard_map.64 = bf16[128,3072]{1,0:T(8,128)(2,1)} custom-call(bf16[128,3072]{1,0:T(8,128)(2,1)} %x_hbm.1, bf16[128,3072]{1,0:T(8,128)(2,1)} %dy_hbm.1, bf16[12,3,256,8,128]{4,3,2,1,0:T(8,128)(2,1)} %bitcast.4, bf16[12,256,8,128]{3,2,1,0:T(8,128)(2,1)} %bitcast.6, bf16[12,256,8,128]{3,2,1,0:T(8,128)(2,1)} %bitcast.7, bf16[8,3,128,3072]{3,2,1,0:T(8,128)(2,1)} %bitcast.5), custom_call_target="tpu_custom_call" | custom-call | tf_op jit(solution)/shard_map/pallas_call | solution.py:269
  64.6 2.1 %copy.8 = bf16[128,3072]{1,0:T(8,128)(2,1)} copy(bf16[128,3072]{1,0:T(8,128)(2,1)} %shard_map.64) | data formatting | bytes 1572864

commit v2 on v1

v2 whole, which is shorter than its diff:
```python
import math

import jax
import jax.numpy as jnp
from jax import lax
from jax.experimental import pallas as pl
from jax.experimental.pallas import tpu as pltpu
from jax.sharding import PartitionSpec as P

MESH = pl.DeviceIdType.MESH
BF16, F32 = jnp.bfloat16, jnp.float32
NT = (((1,), (1,)), ((), ()))

N_DEV, TOK, SEG = 8, 128, 64
SEQ = N_DEV * TOK
D = 3072
HD = 128
HQ, HKV, G = 24, 8, 3
BQ = 256
NB = SEQ // BQ
C = HD**-0.5
C2 = C * math.log2(math.e)
WO_SLOTS, W_SLOTS = 4, 4
RB = 128
U_DO, U_K, U_V, U_Q = 0, 3, 4, 5


scope = jax.named_scope


def dot_nt(a, b):
    return lax.dot_general(a, b, NT, preferred_element_type=F32)


def dot(a, b):
    return jnp.dot(a, b, preferred_element_type=F32)


def kernel(x_hbm, dy_hbm, wq_hbm, wk_hbm, wv_hbm, wo_hbm, out_hbm,
           x_v, dy_v, wo_s, w_s, wrel, sbuf, recv, obuf, rin, acc, res,
           s_scr, dp_scr, p_scr, ds_scr, kt, vt, dk_acc, dv_acc,
           io_sem, wo_sem, w_sem, send_sem, recv_sem, osend_sem, orecv_sem, out_sem):
    me = lax.axis_index("cp")
    dp = lax.axis_index("dp")
    chip = me // 2

    barrier = pltpu.get_barrier_semaphore()
    for p in range(1, N_DEV):
        pl.semaphore_signal(barrier, inc=1, device_id=(dp, lax.rem(me + p, N_DEV)), device_id_type=MESH)

    x_cp = pltpu.make_async_copy(x_hbm, x_v, io_sem.at[0])
    dy_cp = pltpu.make_async_copy(dy_hbm, dy_v, io_sem.at[1])

    def wo_copy(s):
        cc = lax.rem(chip + s % 4 + 1, 4)
        slot = s % WO_SLOTS
        return pltpu.make_async_copy(wo_hbm.at[pl.ds(2 * cc, 2), s // 4], wo_s.at[slot], wo_sem.at[slot])

    def w_copy(w_hbm, i, slot):
        return pltpu.make_async_copy(w_hbm.at[i], w_s.at[slot], w_sem.at[slot])

    dy_cp.start()
    for s in range(WO_SLOTS):
        wo_copy(s).start()
    x_cp.start()
    for i in range(4):
        w_copy(wk_hbm, i, i).start()
    dk_acc[...] = jnp.zeros_like(dk_acc)
    dv_acc[...] = jnp.zeros_like(dv_acc)

    def send_block(unit, dest, val):
        @pl.when(dest != me)
        def _():
            sbuf[unit, dest] = val
            for half, seg in ((0, me), (1, 2 * N_DEV - 1 - me)):
                pltpu.make_async_remote_copy(
                    src_ref=sbuf.at[unit, dest, pl.ds(half * SEG, SEG)],
                    dst_ref=recv.at[unit, pl.ds(pl.multiple_of(seg * SEG, SEG), SEG)],
                    send_sem=send_sem, recv_sem=recv_sem.at[unit],
                    device_id=(dp, dest), device_id_type=MESH).start()

        @pl.when(dest == me)
        def _():
            recv[unit, pl.ds(pl.multiple_of(me * SEG, SEG), SEG), :] = val[:SEG]
            recv[unit, pl.ds(pl.multiple_of((2 * N_DEV - 1 - me) * SEG, SEG), SEG), :] = val[SEG:]

    def send_pair(unit, cc, val):
        for q in range(2):
            send_block(unit, 2 * cc + q, val[:, q * HD:(q + 1) * HD])

    def do_dot(s):
        w = wo_s[s % WO_SLOTS].reshape(2 * HD, D)
        return dot_nt(dy_v[...], w).astype(BF16)

    def do_parts(s):
        acc_v = None
        for k in range(6):
            ks = slice(k * 512, (k + 1) * 512)
            t = dot_nt(dy_v[:, ks], wo_s[s % WO_SLOTS, :, :, ks].reshape(2 * HD, 512))
            acc_v = t if acc_v is None else acc_v + t
            yield acc_v

    def x_parts(h0, h1):
        acc_v = None
        for k in range(6):
            ks = slice(k * 512, (k + 1) * 512)
            t = dot(x_v[:, ks], jnp.concatenate([wrel[h0, ks, :], wrel[h1, ks, :]], axis=1))
            acc_v = t if acc_v is None else acc_v + t
            yield acc_v

    def do_send(s, val):
        send_pair(U_DO + s // 4, lax.rem(chip + s % 4 + 1, 4), val)

        @pl.when(s + WO_SLOTS < 12)
        def _():
            wo_copy(s + WO_SLOTS).start()

    def relay_kv(i, slot):
        base = HQ + 8 * (i // 4)
        for r in range(0, 768, RB):
            row = pl.multiple_of((i % 4) * 768 + r, RB)
            wrel[pl.ds(base, 8), pl.ds(row, RB), :] = jnp.swapaxes(w_s[slot, pl.ds(r, RB)], 0, 1)
            yield

    def relay_q(j, slot):
        for r in range(0, 256, RB):
            row = pl.multiple_of(j * 256 + r, RB)
            blk = w_s[slot, pl.ds(3 * r, 3 * RB)].reshape(RB, 3, 8, HD)
            for t in range(3):
                wrel[pl.ds(8 * t, 8), pl.ds(row, RB), :] = jnp.swapaxes(blk[:, t], 0, 1)
                yield

    def x_dot(h0, h1):
        w = jnp.concatenate([wrel[h0], wrel[h1]], axis=1)
        return dot(x_v[...], w).astype(BF16)

    with scope('dywait'):
        dy_cp.wait()
    with scope('barrier'):
        pl.semaphore_wait(barrier, N_DEV - 1)

    def step_a(s, _):
        wo_copy(s).wait()
        do_send(s, do_dot(s))
        return 0

    with scope('do'):
        lax.fori_loop(0, 4, step_a, 0)

    def step_b(i, _):
        s = i + 4
        slot = i % W_SLOTS
        wo_copy(s).wait()
        w_copy(wk_hbm, 0, slot).wait()
        for val, _ in zip(do_parts(s), relay_kv(i, slot)):
            pass
        val = val.astype(BF16)
        do_send(s, val)

        @pl.when(i < 4)
        def _():
            w_copy(wv_hbm, i, slot).start()

        @pl.when(i >= 4)
        def _():
            w_copy(wq_hbm, i - 4, slot).start()
        return 0

    with scope('do_relkv'):
        lax.fori_loop(0, 8, step_b, 0)
    x_cp.wait()

    def step_c(j, _):
        slot = j % W_SLOTS
        w_copy(wk_hbm, 0, slot).wait()
        cc = lax.rem(chip + j % 4 + 1, 4)
        h0 = HQ + 8 * (j // 4) + 2 * cc
        for val, _ in zip(x_parts(h0, h0 + 1), relay_q(j, slot)):
            pass
        val = val.astype(BF16)
        send_pair(U_K + j // 4, cc, val)
        w_copy(wq_hbm, j + W_SLOTS, slot).start()
        return 0

    with scope('kv_relq'):
        lax.fori_loop(0, 8, step_c, 0)

    def step_d(j, _):
        slot = j % W_SLOTS
        w_copy(wk_hbm, 0, slot).wait()
        for _ in relay_q(j, slot):
            pass
        return 0

    with scope('relq'):
        lax.fori_loop(8, 12, step_d, 0)

    def q_step(s, _):
        g = s // 2
        ccs = [lax.rem(chip + 2 * (s % 2) + k + 1, 4) for k in range(2)]
        vals = [x_dot(6 * cc + g, 6 * cc + g + 3) for cc in ccs]
        for cc, val in zip(ccs, vals):
            send_pair(U_Q + g, cc, val)
        return 0

    with scope('q'):
        lax.fori_loop(0, 6, q_step, 0)

    def wait_unit(u):
        part = recv.at[u, pl.ds(0, SEQ - TOK)]
        pltpu.make_async_copy(part, part, recv_sem.at[u]).wait()

    with scope('waitkv'):
        wait_unit(U_K)
        wait_unit(U_V)
    kt[...] = recv[U_K].T
    vt[...] = recv[U_V].T

    def send_out(u, head, seg):
        dest, half = (seg, 0) if seg < N_DEV else (2 * N_DEV - 1 - seg, 1)
        rows = pl.ds(seg * SEG, SEG)

        @pl.when(dest != me)
        def _():
            pltpu.make_async_remote_copy(
                src_ref=obuf.at[u, rows], dst_ref=rin.at[head, pl.ds(half * SEG, SEG)],
                send_sem=osend_sem, recv_sem=orecv_sem.at[u],
                device_id=(dp, dest), device_id_type=MESH).start()

        @pl.when(dest == me)
        def _():
            rin[head, half * SEG:(half + 1) * SEG, :] = obuf[u, rows, :]

    def attn_head(g, _):
        with scope('waitq'):
            wait_unit(U_DO + g)
            wait_unit(U_Q + g)
        st = [{} for _ in range(NB)]

        def rows_of(b):
            return slice(b * BQ, (b + 1) * BQ)

        def chunks(b):
            return [slice(k * BQ, (k + 1) * BQ) for k in range(b + 1)]

        def scores(b):
            qb = recv[U_Q + g, rows_of(b), :]
            dob = recv[U_DO + g, rows_of(b), :]
            mx = None
            for kc, ks in enumerate(chunks(b)):
                s = dot_nt(recv[U_K, ks, :], qb)
                if kc == b:
                    key = lax.broadcasted_iota(jnp.int32, (BQ, BQ), 0)
                    qry = lax.broadcasted_iota(jnp.int32, (BQ, BQ), 1)
                    s = jnp.where(key <= qry, s, -jnp.inf)
                s_scr[b][ks, :] = s
                mc = jnp.max(s.reshape(BQ // 8, 8, BQ), axis=0)
                mx = mc if mx is None else jnp.maximum(mx, mc)
            for ks in chunks(b):
                dp_scr[b][ks, :] = dot_nt(recv[U_V, ks, :], dob)
            st[b]['m2'] = jnp.max(mx, axis=0, keepdims=True) * C2

        def probs(b):
            m2 = st[b]['m2']
            ls = None
            for ks in chunks(b):
                e = jnp.exp2(s_scr[b][ks, :] * C2 - m2)
                lc = jnp.sum(e.reshape(BQ // 8, 8, BQ), axis=0)
                ls = lc if ls is None else ls + lc
            lse2 = m2 + jnp.log2(jnp.sum(ls, axis=0, keepdims=True))
            for ks in chunks(b):
                p_scr[b][ks, :] = jnp.exp2(s_scr[b][ks, :] * C2 - lse2).astype(BF16)

        def outs(b):
            n = (b + 1) * BQ
            dob = recv[U_DO + g, rows_of(b), :]
            ot = dot(vt[:, :n], p_scr[b][...]).astype(BF16)
            st[b]['delta'] = jnp.sum(dob.T.astype(F32) * ot.astype(F32), axis=0, keepdims=True)
            for ks in chunks(b):
                dv_acc[ks, :] += dot(p_scr[b][ks, :], dob)

        def dscores(b):
            delta = st[b]['delta']
            for ks in chunks(b):
                ds_scr[b][ks, :] = (p_scr[b][ks, :].astype(F32) * (dp_scr[b][ks, :] - delta)).astype(BF16)

        def grads(b):
            n = (b + 1) * BQ
            qb = recv[U_Q + g, rows_of(b), :]
            for ks in chunks(b):
                dk_acc[ks, :] += dot(ds_scr[b][ks, :], qb)
            dqt = (dot(kt[:, :n], ds_scr[b][...]) * C).astype(BF16)
            obuf[g, rows_of(b), :] = dqt.T

        with scope('attn'):
            scores(3)
            scores(2)
            probs(3)
            outs(3)
            scores(1)
            dscores(3)
            probs(2)
            grads(3)
            outs(2)
            scores(0)
            dscores(2)
            probs(1)
            grads(2)
            outs(1)
            dscores(1)
            probs(0)
            grads(1)
            outs(0)
            dscores(0)
            grads(0)

        with scope('send'):
            for seg in range(2 * N_DEV):
                send_out(g, G * me + g, seg)
        return 0

    lax.fori_loop(0, G, attn_head, 0)
    with scope('senddkv'):
        obuf[3] = (dk_acc[...] * C).astype(BF16)
        for seg in range(2 * N_DEV):
            send_out(3, HQ + me, seg)
        obuf[4] = dv_acc[...].astype(BF16)
        for seg in range(2 * N_DEV):
            send_out(4, HQ + HKV + me, seg)

    ND = 1536
    for u in range(5):
        with scope('waito'):
            part = obuf.at[u, pl.ds(0, SEQ - TOK)]
            pltpu.make_async_copy(part, part, orecv_sem.at[u]).wait()
        heads = [G * j + u for j in range(8)] if u < 3 else [HQ + 8 * (u - 3) + j for j in range(8)]

        def dx_step(i, _, u=u, heads=heads):
            cols = pl.ds(pl.multiple_of(i * ND, ND), ND)
            lhs = jnp.concatenate([rin[h] for h in heads], axis=1)
            rhs = jnp.concatenate([wrel[h, cols, :] for h in heads], axis=1)
            t = dot_nt(lhs, rhs)
            if u > 0:
                t = t + acc[:, cols]
            if u < 4:
                acc[:, cols] = t
            else:
                res[:, cols] = t.astype(BF16)
                pltpu.make_async_copy(res.at[:, cols], out_hbm.at[:, cols], out_sem).start()
            return 0

        with scope('dx'):
            lax.fori_loop(0, D // ND, dx_step, 0)

    with scope('final'):
      part = sbuf.at[pl.ds(0, 7)]
      pltpu.make_async_copy(part, part, send_sem).wait()
      part = obuf.at[:, pl.ds(0, SEQ - TOK)]
      pltpu.make_async_copy(part, part, osend_sem).wait()
      pltpu.make_async_copy(res, out_hbm, out_sem).wait()


def solution(mesh):
    row_spec = P(("dp", "cp"), None)

    def device_fn(x_in, d_y, w_q, w_k, w_v, w_o):
        dma = pltpu.SemaphoreType.DMA
        return pl.pallas_call(
            kernel,
            out_shape=jax.ShapeDtypeStruct((TOK, D), BF16),
            in_specs=[pl.BlockSpec(memory_space=pl.ANY)] * 6,
            out_specs=pl.BlockSpec(memory_space=pl.ANY),
            scratch_shapes=[
                pltpu.VMEM((TOK, D), BF16),
                pltpu.VMEM((TOK, D), BF16),
                pltpu.VMEM((WO_SLOTS, 2, HD, D), BF16),
                pltpu.VMEM((W_SLOTS, 768, 8, HD), BF16),
                pltpu.VMEM((HQ + 2 * HKV, D, HD), BF16),
                pltpu.VMEM((8, N_DEV, TOK, HD), BF16),
                pltpu.VMEM((8, SEQ, HD), BF16),
                pltpu.VMEM((5, SEQ, HD), BF16),
                pltpu.VMEM((HQ + 2 * HKV, TOK, HD), BF16),
                pltpu.VMEM((TOK, D), F32),
                pltpu.VMEM((TOK, D), BF16),
                *[[pltpu.VMEM(((b + 1) * BQ, BQ), t) for b in range(NB)] for t in (F32, F32, BF16, BF16)],
                pltpu.VMEM((HD, SEQ), BF16),
                pltpu.VMEM((HD, SEQ), BF16),
                pltpu.VMEM((SEQ, HD), F32),
                pltpu.VMEM((SEQ, HD), F32),
                dma((2,)), dma((WO_SLOTS,)), dma((W_SLOTS,)),
                dma, dma((8,)), dma, dma((5,)), dma,
            ],
            compiler_params=pltpu.CompilerParams(
                collective_id=0, has_side_effects=True, vmem_limit_bytes=67_043_328),
        )(x_in, d_y, w_q.reshape(12, 768, 8, HD), w_k.reshape(4, 768, 8, HD), w_v.reshape(4, 768, 8, HD),
          w_o.reshape(8, 3, HD, D))

    return jax.shard_map(device_fn, mesh=mesh, in_specs=(row_spec, row_spec, P(), P(), P(), P()),
                         out_specs=row_spec, check_vma=False)
```

time: 66.8 us -> 58.6 us (0.88)
  Pallas kernels: 64.6 us -> 56.4 us
    pallas_call x1, Pallas kernels: 64.6 us -> 56.4 us  [device_fn(): pl.pallas_call(kernel, out_shape=jax.ShapeDtypeStruct((TOK, D), BF16), in...]
where the time goes in v2:
time: 58.6 us; the launch traced here: 58.5 us
  Pallas kernels  56.4 us (96%)
  local copies, waits for them, and re-layouts  2.06 us (4%)
    pallas_call x1, Pallas kernels, device_fn(): pl.pallas_call(kernel, out_shape=jax.ShapeDtypeStruct((TOK, D), BF16), in...  56.4 us
    unnamed x1, local copies, waits for them, and re-layouts  2.06 us

profile of v2, /device:TPU:0, one launch (start us, length us, event | category | flops | bytes accessed | tf_op | source)
XLA Modules:
  0.0 58.5 jit_solution(15446090921589776502)
XLA Ops:
  0.0 56.4 %shard_map.64 = bf16[128,3072]{1,0:T(8,128)(2,1)} custom-call(bf16[128,3072]{1,0:T(8,128)(2,1)} %x_hbm.1, bf16[128,3072]{1,0:T(8,128)(2,1)} %dy_hbm.1, bf16[12,768,8,128]{3,2,1,0:T(8,128)(2,1)} %bitcast.4, bf16[4,768,8,128]{3,2,1,0:T(8,128)(2,1)} %bitcast.6, bf16[4,768,8,128]{3,2,1,0:T(8,128)(2,1)} %bitcast.7, bf16[8,3,128,3072]{3,2,1,0:T(8,128)(2,1)} %bitcast.5), custom_call_target="tpu_custom_call" | custom-call | tf_op jit(solution)/shard_map/pallas_call | solution.py:368
  56.4 2.1 %copy.8 = bf16[128,3072]{1,0:T(8,128)(2,1)} copy(bf16[128,3072]{1,0:T(8,128)(2,1)} %shard_map.64) | data formatting | bytes 1572864
